TPU v7x, 16 devices: a whole 2x2x2 slice. The times are simulated.
16 devices in a mesh: dp: 16 (over z, y, x, core).
Axes of the slice: x: 2, y: 2, z: 2, core: 2. Of those that a mesh axis runs over, the one named last changes fastest.
Arguments:
- features: bfloat16 [4096, 256], P('dp')
- w_in: bfloat16 [256, 1024], replicated
- w_out: bfloat16 [1024, 128], replicated
- item_table: bfloat16 [262144, 128], P('dp')
- cand_ids: int32 [16384], replicated
- log_q: float32 [16384], replicated
- targets: int32 [4096], P('dp')
Outputs:
- output 1: float32 [], replicated
- output 2: float32 [262144, 128], P('dp')
- output 3: float32 [256, 1024], replicated
- output 4: float32 [1024, 128], replicated
All inputs are finite; a program needn't handle non-finite values.
Results may differ from a plain program's by a relative error of at most 0.001.
Values are sent between devices in bfloat16 or wider.
A program may use at most 1 GiB of HBM per device.

v0:
```python
import jax
import jax.numpy as jnp
from jax import lax
from jax.sharding import PartitionSpec as P


def solution(mesh):
    num_dev = mesh.shape["dp"]

    def local_step(features, w_in, w_out, table_blk, cand_ids, log_q, targets):
        dev_index = lax.axis_index("dp")
        block_rows = table_blk.shape[0]
        cand_dev = cand_ids.shape[0] // num_dev
        tok_total = features.shape[0] * num_dev
        pre_act = jnp.dot(features, w_in, preferred_element_type=jnp.float32)
        act_val, gelu_back = jax.vjp(jax.nn.gelu, pre_act)
        act_b = act_val.astype(jnp.bfloat16)
        query = jnp.dot(act_b, w_out, preferred_element_type=jnp.float32).astype(jnp.bfloat16)
        query_all = lax.all_gather(query, "dp", axis=0, tiled=True)
        tgt_all = lax.all_gather(targets, "dp", axis=0, tiled=True)
        row_base = dev_index * block_rows
        tgt_local = tgt_all - row_base
        tgt_own = (tgt_local >= 0) & (tgt_local < block_rows)
        tgt_index = jnp.clip(tgt_local, 0, block_rows - 1)
        tgt_rows = table_blk[tgt_index]
        own_cands = lax.dynamic_slice_in_dim(cand_ids, dev_index * cand_dev, cand_dev)
        own_logq = lax.dynamic_slice_in_dim(log_q, dev_index * cand_dev, cand_dev)
        cand_index = own_cands - row_base
        cand_rows = table_blk[cand_index]
        tgt_dot = jnp.einsum("td,td->t", query_all, tgt_rows, preferred_element_type=jnp.float32)
        tgt_logit = lax.psum(jnp.where(tgt_own, tgt_dot, 0.0), "dp")
        cand_logit = jnp.einsum("td,cd->tc", query_all, cand_rows, preferred_element_type=jnp.float32) - own_logq[None, :]
        cand_logit = jnp.where(own_cands[None, :] == tgt_all[:, None], -1e9, cand_logit)
        top_val = jnp.maximum(lax.pmax(jnp.max(cand_logit, axis=1), "dp"), tgt_logit)
        exp_sum = lax.psum(jnp.sum(jnp.exp(cand_logit - top_val[:, None]), axis=1), "dp")
        log_norm = top_val + jnp.log(exp_sum + jnp.exp(tgt_logit - top_val))
        loss = jnp.sum(log_norm - tgt_logit) / tok_total
        grad_tgt = (jnp.exp(tgt_logit - log_norm) - 1.0) / tok_total
        cand_grad = (jnp.exp(cand_logit - log_norm[:, None]) / tok_total).astype(jnp.bfloat16)
        own_grad = jnp.where(tgt_own, grad_tgt, 0.0)
        dq_part = own_grad[:, None] * tgt_rows + jnp.einsum("tc,cd->td", cand_grad, cand_rows, preferred_element_type=jnp.float32)
        dq_local = lax.psum_scatter(dq_part, "dp", scatter_dimension=0, tiled=True).astype(jnp.bfloat16)
        grad_cand = jnp.einsum("tc,td->cd", cand_grad, query_all, preferred_element_type=jnp.float32)
        grad_blk = jnp.zeros(table_blk.shape, jnp.float32).at[cand_index].add(grad_cand).at[tgt_index].add(own_grad[:, None] * query_all)
        d_act = jnp.einsum("td,fd->tf", dq_local, w_out, preferred_element_type=jnp.float32)
        d_pre = gelu_back(d_act)[0].astype(jnp.bfloat16)
        grad_w_out = lax.psum(jnp.einsum("tf,td->fd", act_b, dq_local, preferred_element_type=jnp.float32), "dp")
        grad_w_in = lax.psum(jnp.einsum("ti,tf->if", features, d_pre, preferred_element_type=jnp.float32), "dp")
        return loss, grad_blk, grad_w_in, grad_w_out

    return jax.shard_map(local_step, mesh=mesh, in_specs=(P("dp", None), P(), P(), P("dp", None), P(), P(), P("dp")), out_specs=(P(), P("dp", None), P(), P()), check_vma=False)
```

profile of v0, /device:TPU:0, one launch (start us, length us, event | category | flops | bytes accessed | tf_op | source)
XLA Modules:
  0.0 322.3 jit_solution(550271515576839533)
XLA Ops:
  7.2 0.0 copy-start
  7.2 0.0 all-gather.3.cloned.1.call-start
  7.2 1.0 copy-done
  8.2 1.2 fusion.32
  9.4 2.1 convolution_convert_fusion
  11.5 0.0 all-gather.3.cloned.1.call-update
  11.5 0.0 reduce-scatter.2.cloned.1.call-start
  11.6 0.7 dynamic_slice.7
  12.2 0.7 broadcast_clamp_fusion.1
  12.9 5.6 %gather_fusion = bf16[1024,128]{1,0:T(8,128)(2,1)S(1)} fusion(bf16[16384,128]{1,0:T(8,128)(2,1)} %param.10, s32[1024]{0:T(1024)S(1)} %get-tuple-element.24), kind=kCustom, calls=%fused_computation | custom fusion | bytes 528384 | tf_op jit(solution)/shard_map/gather | solution.py:29
  18.6 14.5 %all-gather = s32[16,1,256]{2,1,0:T(1,128)S(1)} all-gather(s32[1,1,256]{2,1,0:T(1,128)} %bitcast.20), channel_id=1, replica_groups=mesh['dp'=16] {'dp'}, dimensions={0}, use_global_device_ids=true | all-gather | bytes 17408 | tf_op jit(solution)/shard_map/all_gather | solution.py:20
  33.1 13.8 %gather_fusion.1 = bf16[4096,128]{1,0:T(8,128)(2,1)S(1)} fusion(bf16[16384,128]{1,0:T(8,128)(2,1)} %param.10, s32[4096]{0:T(1024)S(1)} %get-tuple-element.22), kind=kCustom, calls=%fused_computation.1 | custom fusion | bytes 2113536 | tf_op jit(solution)/shard_map/gather | solution.py:25
  46.9 0.0 all-gather.3.cloned.1.call-done
  46.9 1.8 fusion.3
  48.7 31.9 %psum.28 = f32[4096]{0:T(1024)S(1)} all-reduce(f32[4096]{0:T(1024)S(1)} %get-tuple-element.20), channel_id=1, replica_groups=mesh['dp'=16] {'dp'}, use_global_device_ids=true, to_apply=%region_2.3 | all-reduce | flops 4096 | bytes 32768 | tf_op jit(solution)/shard_map/psum | solution.py:31
  80.6 8.2 %fusion = (f32[4096]{0:T(1024)S(1)}, f32[4096,1024]{0,1:T(8,128)}) fusion(f32[1024]{0:T(1024)S(1)} %dynamic_slice.7, s32[4096]{0:T(1024)S(1)} %bitcast.17, s32[1024]{0:T(1024)S(1)} %get-tuple-element.26, bf16[4096,128]{1,0:T(8,128)(2,1)} %all-gather.3.cloned.1.call-done, bf16[1024,128]{1,0:T(8,128)(2,1)S(1)} %gather_fusion), kind=kOutput, calls=%fused_computation.7 | convolution fusion | flops 1090514944 | bytes 18128896 | tf_op jit(solution)/shard_map/td,cd->tc/dot_general | solution.py:32
  88.9 32.7 %pmax.7 = f32[4096]{0:T(1024)S(1)} all-reduce(f32[4096]{0:T(1024)S(1)} %get-tuple-element.27), channel_id=1, replica_groups=mesh['dp'=16] {'dp'}, use_global_device_ids=true, to_apply=%region_1.2 | all-reduce | flops 4096 | bytes 32768 | tf_op jit(solution)/shard_map/pmax | solution.py:34
  121.5 8.1 %exponential_reduce_fusion = f32[4096]{0:T(1024)S(1)} fusion(f32[4096,1024]{0,1:T(8,128)} %get-tuple-element.28, f32[4096]{0:T(1024)S(1)} %max.9, f32[1024]{0:T(1024)S(1)} %dynamic_slice.7, s32[4096]{0:T(1024)S(1)} %bitcast.18, s32[1024]{0:T(1024)S(1)} %get-tuple-element.26), kind=kLoop, calls=%fused_computation.5 | loop fusion | flops 20967424 | bytes 16834560 | tf_op jit(solution)/shard_map/reduce_sum | solution.py:35
  129.7 32.9 %psum.29 = f32[4096]{0:T(1024)S(1)} all-reduce(f32[4096]{0:T(1024)S(1)} %exponential_reduce_fusion), channel_id=1, replica_groups=mesh['dp'=16] {'dp'}, use_global_device_ids=true, to_apply=%region_4.5 | all-reduce | flops 4096 | bytes 32768 | tf_op jit(solution)/shard_map/psum | solution.py:35
  162.7 8.6 %multiply_convert_fusion = bf16[4096,1024]{0,1:T(8,128)(2,1)S(1)} fusion(f32[4096,1024]{0,1:T(8,128)} %get-tuple-element.28, f32[4096]{0:T(1024)S(1)} %get-tuple-element.19, f32[1024]{0:T(1024)S(1)} %dynamic_slice.7, s32[4096]{0:T(1024)S(1)} %bitcast.19, s32[1024]{0:T(1024)S(1)} %get-tuple-element.26), kind=kLoop, calls=%fused_computation.4 | loop fusion | flops 25165824 | bytes 25206784 | tf_op jit(solution)/shard_map/convert_element_type | solution.py:39
  171.3 0.0 copy-start.1
  171.3 3.4 %copy-done.1 = bf16[4096,1024]{0,1:T(8,128)(2,1)} copy-done((bf16[4096,1024]{0,1:T(8,128)(2,1)}, bf16[4096,1024]{0,1:T(8,128)(2,1)S(1)}, u32[]{:S(2)}) %copy-start.1) | copy-done | bytes 8388632
  174.7 0.0 copy-start.3
  174.7 0.0 copy-start.4
  174.7 4.2 %convolution_add_fusion = f32[4096,128]{1,0:T(8,128)} fusion(bf16[4096,1024]{0,1:T(8,128)(2,1)S(1)} %multiply_convert_fusion, bf16[1024,128]{1,0:T(8,128)(2,1)S(1)} %gather_fusion, bf16[4096,128]{1,0:T(8,128)(2,1)S(1)} %gather_fusion.1, f32[4096]{0:T(1024)S(1)} %get-tuple-element.18), kind=kOutput, calls=%fused_computation.8 | convolution fusion | flops 1075314688 | bytes 11812864 | tf_op jit(solution)/shard_map/tc,cd->td/dot_general | solution.py:41
  178.8 0.0 copy-start.2
  178.8 0.0 reduce-scatter.2.cloned.1.call-update
  178.8 0.0 all-reduce.3.cloned.1.call-start
  178.9 58.5 %reduce-scatter.2.cloned.1.call-done = f32[256,128]{1,0:T(8,128)} async-done(((f32[4096,128]{1,0:T(8,128)}), f32[256,128]{1,0:T(8,128)}) %reduce-scatter.2.cloned.1.call-update) | async-done | bytes 131088 | tf_op jit(solution)/shard_map/reduce_scatter | solution.py:42
  237.4 2.3 fusion.22
  239.6 0.0 copy-done.3
  239.6 0.0 copy-done.4
  239.6 2.9 convolution_bitcast_fusion
  242.6 0.0 all-reduce.3.cloned.1.call-update
  242.6 0.6 subtract_reduce_fusion
  243.9 0.0 copy-done.2
  243.9 5.7 %fusion.33 = f32[1024,128]{1,0:T(8,128)S(1)} fusion(bf16[4096,1024]{0,1:T(8,128)(2,1)} %copy-done.1, bf16[4096,128]{1,0:T(8,128)(2,1)S(1)} %copy-done.2), kind=kOutput, calls=%fused_computation.56 | convolution fusion | flops 1073741824 | bytes 9961472 | tf_op jit(solution)/shard_map/tc,td->cd/dot_general | solution.py:43
  249.6 9.9 %scatter_custom_fusion = f32[16384,128]{1,0:T(8,128)} fusion(s32[1024]{0:T(1024)S(1)} %get-tuple-element.25, f32[1024,128]{1,0:T(8,128)S(1)} %fusion.33, f32[]{:T(128)} %constant.10.clone.1), kind=kCustom, calls=%fused_computation.9 | custom fusion | flops 131072 | bytes 8388612 | tf_op jit(solution)/shard_map/scatter-add | solution.py:44
  259.5 34.3 %scatter_custom_fusion.1 = f32[16384,128]{1,0:T(8,128)} fusion(f32[16384,128]{1,0:T(8,128)} %scatter_custom_fusion, s32[4096]{0:T(1024)S(1)} %get-tuple-element.23, bf16[4096,128]{1,0:T(8,128)(2,1)S(1)} %copy-done.2, f32[4096]{0:T(1024)S(1)} %get-tuple-element.18), kind=kCustom, calls=%fused_computation.15 | custom fusion | flops 1572864 | bytes 9453568 | tf_op jit(solution)/shard_map/scatter-add | solution.py:44
  293.7 16.5 %all-reduce.3.cloned.1.call-done = (f32[256,1024]{0,1:T(8,128)}, f32[1024,128]{1,0:T(8,128)}) async-done(((f32[256,1024]{0,1:T(8,128)}, f32[1024,128]{1,0:T(8,128)}), (f32[256,1024]{0,1:T(8,128)}, f32[1024,128]{1,0:T(8,128)})) %all-reduce.3.cloned.1.call-update) | async-done | bytes 1572880 | tf_op jit(solution)/shard_map/psum | solution.py:48
  310.2 2.5 copy.13
  312.7 1.9 copy.22
  (4 shorter events, 0.0 us)
Async XLA Ops:
  7.2 1.0 copy-start
  7.2 39.7 %all-gather.3.cloned.1.call-start = ((), (), s32[]{:S(2)}) async-start(), calls=%async_computation.1 | async-start | bytes 1114112 | tf_op jit(solution)/shard_map/all_gather | solution.py:19
  11.5 225.9 %reduce-scatter.2.cloned.1.call-start = ((), (), s32[]{:S(2)}) async-start(), calls=%async_computation.2 | async-start | bytes 2228224 | tf_op jit(solution)/shard_map/reduce_scatter | solution.py:42
  171.3 3.4 %copy-start.1 = (bf16[4096,1024]{0,1:T(8,128)(2,1)}, bf16[4096,1024]{0,1:T(8,128)(2,1)S(1)}, u32[]{:S(2)}) copy-start(bf16[4096,1024]{0,1:T(8,128)(2,1)S(1)} %multiply_convert_fusion) | copy-start | bytes 25165828
  174.7 65.0 %copy-start.3 = (bf16[256,256]{1,0:T(8,128)(2,1)S(1)}, bf16[256,256]{1,0:T(8,128)(2,1)}, u32[]{:S(2)}) copy-start(bf16[256,256]{1,0:T(8,128)(2,1)} %param.7) | copy-start | bytes 393220
  174.7 65.0 %copy-start.4 = (bf16[1024,128]{1,0:T(8,128)(2,1)S(1)}, bf16[1024,128]{1,0:T(8,128)(2,1)}, u32[]{:S(2)}) copy-start(bf16[1024,128]{1,0:T(8,128)(2,1)} %param.9) | copy-start | bytes 786436
  178.8 65.0 %copy-start.2 = (bf16[4096,128]{1,0:T(8,128)(2,1)S(1)}, bf16[4096,128]{1,0:T(8,128)(2,1)}, u32[]{:S(2)}) copy-start(bf16[4096,128]{1,0:T(8,128)(2,1)} %all-gather.3.cloned.1.call-done) | copy-start | bytes 3145732
  178.8 131.4 %all-reduce.3.cloned.1.call-start = ((), (), s32[]{:S(2)}) async-start(), calls=%async_computation.3 | async-start | bytes 3145728 | tf_op jit(solution)/shard_map/psum | solution.py:48
Sparse Core Ops, SparseCore 0:
  11.6 28.2 all-gather.2
  179.0 58.3 reduce-scatter.1
  242.7 67.4 all-reduce.2
where the time goes:
time: 323 us; the launch traced here: 322 us
  blocking collectives  112 us (35%)
  waiting for transfers between devices  75 us (23%)
  other arithmetic  64.1 us (20%)
  local copies, waits for them, and re-layouts  28.8 us (9%)
  matrix products  26.6 us (8%)
  between operations  15.6 us (5%)
    reduce_scatter x1, waiting for transfers between devices, local_step(): lax.psum_scatter(dq_part, 'dp', scatter_dimension=0, tiled=True)  58.5 us
    scatter-add x2, other arithmetic, local_step(): jnp.zeros(table_blk.shape, jnp.float32).at[cand_index].add(grad_cand)  44.2 us
    psum x1, blocking collectives, local_step(): lax.psum(jnp.sum(jnp.exp(cand_logit - top_val[:, None]), axis=1), 'dp')  32.9 us
    pmax x1, blocking collectives, local_step(): lax.pmax(jnp.max(cand_logit, axis=1), 'dp')  32.7 us
    psum x1, blocking collectives, local_step(): tgt_logit = lax.psum(jnp.where(tgt_own, tgt_dot, 0.0), 'dp')  31.9 us
    psum x1, waiting for transfers between devices, local_step(): lax.psum(jnp.einsum('ti,tf->if', features, d_pre, preferred_element_type=...  16.5 us
    all_gather x1, blocking collectives, local_step(): tgt_all = lax.all_gather(targets, 'dp', axis=0, tiled=True)  14.5 us
    gather x1, local copies, waits for them, and re-layouts, local_step(): tgt_rows = table_blk[tgt_index]  13.8 us
  transfers between devices with their start and end apart: 3, of which 2 were waited for; matrix products, arithmetic and copies ran while one was open for 22% of the time, Pallas kernels for 0%

commit v1 on v0

v1 whole, which is shorter than its diff:
```python
import jax
import jax.numpy as jnp
from jax import lax
from jax.experimental import pallas as pl
from jax.experimental.pallas import tpu as pltpu
from jax.sharding import PartitionSpec as P

F32 = jnp.float32
BF16 = jnp.bfloat16
I32 = jnp.int32
MESH = pl.DeviceIdType.MESH

CORES = 2
CHIPS = 8
DEVS = 16
LANES = 128
TOK = 256
HALF = 128
GRP = 2048
CAND = 1024
PAIR = 2048
CROW = 8
EMB = 128
HID = 1024
IN = 256
ROWS = 16384
TOTAL = 4096
KC = 256
STEPS = PAIR // KC
HB = 256
HSTEPS = HID // HB
ROOT_2_PI = 0.7978845608028654
CUBE = 0.044715
SHARE = 1.0 / TOTAL
VMEM_LIMIT = 64 * 1024 * 1024 - 65536

NEAR = (1, 2, 4, 3, 5, 6, 7)
FAR = (7, 6, 5, 3, 4, 2, 1)


def dot_nt(lhs, rhs):
    return lax.dot_general(lhs, rhs, (((1,), (1,)), ((), ())), preferred_element_type=F32)


def dot_nn(lhs, rhs):
    return jnp.dot(lhs, rhs, preferred_element_type=F32)


def column_of(row):
    return jnp.broadcast_to(row, (LANES, LANES)).T


def top_of(x):
    return jnp.max(x, axis=0, keepdims=True)


def sum_of(x):
    return jnp.sum(x, axis=0, keepdims=True)


def part(i, size):
    return pl.ds(pl.multiple_of(i * size, size), size)


def row(i):
    return pl.ds(i, 1)


def tanh_of(act):
    return jnp.tanh(ROOT_2_PI * (act + CUBE * (act * act * act)))


def main_kernel(
    x_ref, w_in_ref, w_out_ref, tgt_ref, cand_hbm, logq_hbm, table_hbm,
    loss_out, gcand_out, gh_out, idx_out, bounds_out, dwin_out, dwout_out,
    tab_b, tab_f, tall, idx_vm, idx_sm, cand_vm, logq_vm, xs_all, xt_ref, u_ref, hall,
    rows_f, cand_f, e_all, e_t, cid_b, lq_b, trow_s, trow_o, tr_t,
    ex_ref, st_all, mloc_ref, z_ref, l_ref, f_ref, g_ref, gh_ref,
    dh_acc, dh_in, dhb_all, da_ref, de_acc, de_in, gwin, gwout, swin, swout, loss_all, bounds_vm,
    tgt_s, tgt_r, h_s, h_r, x_s, x_r, e_s, e_r, tr_s, tr_r, st_s, st_r, dh_s, dh_r, de_s, de_r, gh_s, gh_r,
    db_s, db_r, wi_s, wi_r, wo_s, wo_r, ls_s, ls_r, loc,
):
    me = lax.axis_index("dp")
    chip = me // CORES
    core = me % CORES
    oth = 1 - core
    sib = chip * CORES + oth
    base = me * ROWS
    first_row = chip * (CORES * ROWS)

    def flip(k):
        out = 0
        for bit in (1, 2, 4):
            out = out + (((chip // bit) + (k // bit)) % 2) * bit
        return out

    peers = {k: flip(k) for k in NEAR}

    def slot_of(device):
        return (device % CORES) * CHIPS + device // CORES

    def rcopy(src, dst, ssem, rsem, dev):
        return pltpu.make_async_remote_copy(src_ref=src, dst_ref=dst, send_sem=ssem, recv_sem=rsem, device_id=(dev,), device_id_type=MESH)

    sent = []

    def go(copy):
        copy.start()
        sent.append(copy)
        return copy

    def swap(src, dst, ssem, rsem):
        return go(rcopy(src, dst, ssem, rsem, sib))

    def arrivals(ref, ssem, rsem):
        return {k: rcopy(ref.at[src], ref.at[src], ssem.at[k], rsem.at[src], src * CORES + core) for k, src in peers.items()}

    def spread(ref, ssem, rsem, ks):
        got = arrivals(ref, ssem, rsem)
        for k in ks:
            go(rcopy(ref.at[chip], ref.at[chip], ssem.at[k], rsem.at[chip], peers[k] * CORES + core))
        return got

    def to_all(ref, slot, ssem, rsem, slots):
        got = []
        for i in range(DEVS - 1):
            src = slots(lax.rem(me + (DEVS - 1) - i, DEVS))
            got.append(rcopy(ref.at[src], ref.at[src], ssem.at[i], rsem.at[src], others[i]))
        for i, dev in enumerate(others):
            go(rcopy(ref.at[slot], ref.at[slot], ssem.at[i], rsem.at[slot], dev))
        return got

    others = [lax.rem(me + k, DEVS) for k in range(1, DEVS)]

    barrier = pltpu.get_barrier_semaphore()
    for dev in others:
        pl.semaphore_signal(barrier, inc=1, device_id=(dev,), device_id_type=MESH)

    chip_blocks = pl.ds(chip * CORES, CORES)
    early = [
        pltpu.make_async_copy(cand_hbm.at[chip_blocks], cand_vm, loc.at[0]),
        pltpu.make_async_copy(logq_hbm.at[chip_blocks], logq_vm, loc.at[1]),
        pltpu.make_async_copy(table_hbm, tab_b, loc.at[2]),
    ]
    for c in early:
        c.start()

    lane = lax.broadcasted_iota(I32, (1, LANES), 1)
    halves = range(TOK // HALF)
    tgt = [tgt_ref[q:q + 1, :] for q in halves]
    key = [tgt[q] * TOK + (lane + q * HALF) for q in halves]
    key_col = [column_of(k) for k in key]
    sub = lax.broadcasted_iota(I32, (TOK, LANES), 0)
    hot = [sub == sum(sum_of((key_col[r] < key[q]).astype(I32)) for r in halves) for q in halves]
    perm = jnp.concatenate([jnp.where(h, 1.0, 0.0).astype(BF16) for h in hot], axis=1)
    moved = [jnp.where(hot[q], jnp.broadcast_to(tgt[q].astype(F32), (TOK, LANES)), 0.0) for q in halves]
    my_slot = core * CHIPS + chip
    for r in halves:
        line = sum(sum_of(m[r * HALF:(r + 1) * HALF, :].T) for m in moved)
        tall[row(my_slot), row(r), :] = line.astype(I32).reshape(1, 1, LANES)

    pl.semaphore_wait(barrier, DEVS - 1)
    tgt_got = to_all(tall, my_slot, tgt_s, tgt_r, slot_of)

    xs = dot_nn(perm, x_ref[...]).astype(BF16)
    xs_all[row(chip)] = xs.reshape(1, TOK, IN)
    act = dot_nn(xs, w_in_ref[...])
    u_ref[...] = (act * (0.5 * (1.0 + tanh_of(act)))).astype(BF16)
    hall[row(chip)] = dot_nn(u_ref[...], w_out_ref[...]).astype(BF16).reshape(1, TOK, EMB)
    h_got = spread(hall, h_s, h_r, NEAR)
    x_got = spread(xs_all, x_s, x_r, NEAR)

    for c in early:
        c.wait()
    for r in range(CROW):
        idx_vm[DEVS + r // 2, r % 2:r % 2 + 1, :] = jnp.clip(cand_vm[core, r:r + 1, :] - base, 0, ROWS - 1)
    cand_at = pl.ds(DEVS, CROW // 2)
    cand_copy = pltpu.make_async_copy(idx_vm.at[cand_at], idx_sm.at[cand_at], loc.at[0])
    cand_copy.start()

    @pl.loop(0, ROWS // KC)
    def _(i):
        tab_f[part(i, KC), :] = tab_b[part(i, KC), :].astype(F32)

    tab_f[pl.ds(ROWS, CROW), :] = jnp.zeros((CROW, EMB), F32)
    cand_copy.wait()

    def gather_rows(slot, dst, first):
        for v in range(TOK):
            dst[row(first + v), :] = tab_f[row(idx_sm[slot, v // LANES, v % LANES]), :]

    @pl.loop(0, CAND // TOK)
    def _(i):
        gather_rows(DEVS + i, cand_f, i * TOK)

    e_all[row(core)] = cand_f[...].astype(BF16).reshape(1, CAND, EMB)
    e_copy = swap(e_all.at[core], e_all.at[core], e_s, e_r)

    for c in tgt_got:
        c.wait_recv()
    loc_idx = tall[...] - base
    own = (loc_idx >= 0) & (loc_idx < ROWS)
    idx_vm[0:DEVS] = jnp.where(own, loc_idx, ROWS)

    def count(mask):
        return jnp.sum(jnp.sum(mask.astype(F32), axis=2, keepdims=True), axis=1, keepdims=True)

    lane3 = lax.broadcasted_iota(I32, (DEVS, 1, LANES), 2)
    bounds_vm[...] = jnp.where(lane3 == 0, count(loc_idx < 0), count(loc_idx < ROWS)).astype(I32)
    tok_at = pl.ds(0, DEVS)
    idx_copy = pltpu.make_async_copy(idx_vm.at[tok_at], idx_sm.at[tok_at], loc.at[0])
    idx_copy.start()
    idx_copy.wait()

    @pl.loop(0, CHIPS)
    def _(q):
        gather_rows(oth * CHIPS + q, rows_f, q * TOK)

    trow_s[...] = rows_f[...].astype(BF16)
    tr_copy = swap(trow_s, trow_o, tr_s, tr_r)

    @pl.loop(0, CHIPS)
    def _(q):
        gather_rows(core * CHIPS + q, rows_f, q * TOK)

    for b in range(CORES):
        for r in range(CROW):
            at = b * CAND + r * LANES
            cid_b[at:at + LANES, :] = column_of(cand_vm[b, r:r + 1, :])
            lq_b[at:at + LANES, :] = column_of(logq_vm[b, r:r + 1, :])
    e_copy.wait_recv()
    for i in range(STEPS):
        b, r = i // (CAND // KC), i % (CAND // KC)
        e_t[:, i * KC:(i + 1) * KC] = e_all[b, r * KC:(r + 1) * KC, :].T
    tr_copy.wait_recv()

    def twice(x):
        return jnp.concatenate([x, x], axis=1)

    def fold(x):
        return x.reshape(KC // 8, 8, TOK)

    def stats_of(q):
        h = hall[q]
        ids = tall[core * CHIPS + q]
        y_row = jnp.concatenate([ids[r:r + 1, :] for r in halves], axis=1)

        def first(i, top):
            e_blk = e_all[i // (CAND // KC), part(i % (CAND // KC), KC), :]
            s = dot_nt(e_blk, h) - twice(lq_b[part(i, KC), :])
            s = jnp.where(twice(cid_b[part(i, KC), :]) == y_row, -1e9, s)
            ex_ref[q, part(i, KC), :] = s
            return jnp.maximum(top, jnp.max(fold(s), axis=0))

        top = top_of(lax.fori_loop(0, STEPS, first, jnp.full((8, TOK), -jnp.inf, F32)))

        def second(i, tot):
            e = jnp.exp(ex_ref[q, part(i, KC), :] - top)
            ex_ref[q, part(i, KC), :] = e
            return tot + jnp.sum(fold(e), axis=0)

        tot = sum_of(lax.fori_loop(0, STEPS, second, jnp.zeros((8, TOK), F32)))
        rows = rows_f[part(q, TOK), :] + trow_o[part(q, TOK), :].astype(F32)
        tr_t[q] = rows.T
        z = sum_of((rows * h.astype(F32)).T)
        mine = (y_row >= first_row) & (y_row < first_row + CORES * ROWS)
        z_ref[row(q), :] = jnp.where(mine, z, 0.0)
        both = jnp.where(mine, jnp.maximum(top, z), top)
        tot = tot * jnp.exp(top - both) + jnp.where(mine, jnp.exp(jnp.where(mine, z - both, 0.0)), 0.0)
        mloc_ref[row(q), :] = top
        st_all[row(chip), 0, row(q), :] = both.reshape(1, 1, TOK)
        st_all[row(chip), 1, row(q), :] = tot.reshape(1, 1, TOK)

    stats_of(chip)
    for k in NEAR:
        h_got[k].wait_recv()
        stats_of(peers[k])
    st_got = spread(st_all, st_s, st_r, FAR)

    def tower_of(q):
        x = xs_all[q]
        xt_ref[:, part(q, TOK)] = x.T

        def step(i, carry):
            act = dot_nn(x, w_in_ref[:, part(i, HB)])
            tanh = tanh_of(act)
            cdf = 0.5 * (1.0 + tanh)
            slope = cdf + act * (0.5 * (1.0 - tanh * tanh)) * (ROOT_2_PI * (1.0 + 3.0 * CUBE * (act * act)))
            u_t = (act * cdf).T.astype(BF16)
            for r in halves:
                at = (q * HSTEPS + i) * 2 + r
                tab_f[part(at, TOK), :] = slope[:, r * HALF:(r + 1) * HALF]
                tab_b[part(at, HB), :] = u_t[:, r * HALF:(r + 1) * HALF]
            return carry

        lax.fori_loop(0, HSTEPS, step, 0)

    tower_of(chip)
    for k in NEAR[:3]:
        x_got[k].wait_recv()
        tower_of(peers[k])

    for k in NEAR:
        st_got[k].wait_recv()
    top_all = st_all[0, 0]
    for c in range(1, CHIPS):
        top_all = jnp.maximum(top_all, st_all[c, 0])
    tot_all = sum(st_all[c, 1] * jnp.exp(st_all[c, 0] - top_all) for c in range(CHIPS))
    log_norm = top_all + jnp.log(tot_all)
    l_ref[...] = log_norm
    f_ref[...] = jnp.exp(mloc_ref[...] - log_norm) * SHARE
    group = pl.ds(core * CHIPS, CHIPS)
    t_all = jnp.concatenate([tall[group, r, :] for r in halves], axis=1)
    mine_all = (t_all >= first_row) & (t_all < first_row + CORES * ROWS)
    z_all = z_ref[...]
    g_ref[...] = jnp.where(mine_all, (jnp.exp(jnp.where(mine_all, z_all - log_norm, 0.0)) - 1.0) * SHARE, 0.0)
    loss_all[row(me)] = (l_ref[row(chip), :] - sum_of(z_all)).reshape(1, 1, TOK)
    ls_got = to_all(loss_all, me, ls_s, ls_r, lambda device: device)

    def grads_of(q, is_first):
        h = hall[q]
        f_row = f_ref[row(q), :]

        def body(i, acc):
            p = (ex_ref[q, part(i, KC), :] * f_row).astype(BF16)
            de = dot_nn(p, h)
            if is_first:
                de_acc[part(i, KC), :] = de
            else:
                de_acc[part(i, KC), :] += de
            return acc + dot_nn(e_t[:, part(i, KC)], p)

        dh_acc[q] = lax.fori_loop(0, STEPS, body, g_ref[row(q), :] * tr_t[q])

    dh_got = arrivals(dh_in, dh_s, dh_r)
    for k in FAR:
        grads_of(peers[k], k == FAR[0])
        go(rcopy(dh_acc.at[peers[k]], dh_in.at[chip], dh_s.at[k], dh_r.at[chip], peers[k] * CORES + core))
    grads_of(chip, False)
    de_copy = swap(de_acc.at[part(oth, CAND), :], de_in, de_s, de_r)

    @pl.loop(0, CHIPS)
    def _(q):
        g_row = g_ref[row(q), :]
        for r in halves:
            col = column_of(g_row[:, r * HALF:(r + 1) * HALF])
            gh_ref[part((core * CHIPS + q) * 2 + r, HALF), :] = col * hall[q, r * HALF:(r + 1) * HALF, :].astype(F32)

    gh_copy = swap(gh_ref.at[part(core, GRP), :], gh_ref.at[part(core, GRP), :], gh_s, gh_r)

    for k in NEAR[3:]:
        x_got[k].wait_recv()
        tower_of(peers[k])

    de_copy.wait_recv()
    for r in range(CAND // KC):
        cand_f[r * KC:(r + 1) * KC, :] = de_acc[part(core * (CAND // KC) + r, KC), :] + de_in[r * KC:(r + 1) * KC, :]
    for c in ls_got:
        c.wait_recv()
    loss_out[...] = jnp.sum(jnp.sum(loss_all[...], axis=0), axis=1, keepdims=True) * SHARE
    gh_copy.wait_recv()
    outs = [
        pltpu.make_async_copy(gh_ref, gh_out, loc.at[0]),
        pltpu.make_async_copy(idx_vm, idx_out, loc.at[1]),
        pltpu.make_async_copy(bounds_vm, bounds_out, loc.at[2]),
        pltpu.make_async_copy(cand_f, gcand_out, loc.at[3]),
    ]
    for c in outs:
        c.start()

    for k in NEAR:
        dh_got[k].wait_recv()
    total = dh_acc[chip]
    for k in NEAR:
        total = total + dh_in[peers[k]]
    dhb_all[row(chip)] = total.T.astype(BF16).reshape(1, TOK, EMB)
    db_got = spread(dhb_all, db_s, db_r, FAR)

    def back_of(q):
        dh = dhb_all[q]

        def step(i, carry):
            e = dot_nt(dh, w_out_ref[part(i, HB), :])
            slope = [tab_f[part((q * HSTEPS + i) * 2 + r, TOK), :] for r in halves]
            da_ref[part(q, TOK), part(i, HB)] = (jnp.concatenate(slope, axis=1) * e).astype(BF16)
            return carry

        lax.fori_loop(0, HSTEPS, step, 0)

    back_of(chip)
    for k in FAR:
        db_got[k].wait_recv()
        back_of(peers[k])

    w_got = []
    for i in range(HSTEPS):
        gwin[i] = dot_nn(xt_ref[...], da_ref[:, i * HB:(i + 1) * HB])
        w_got.append(swap(gwin.at[i], swin.at[i], wi_s.at[i], wi_r.at[i]))
    dh_flat = dhb_all[...].reshape(GRP, EMB)
    for i in range(HSTEPS):
        u_t = jnp.concatenate([tab_b[((q * HSTEPS + i) * 2 + r) * HB:((q * HSTEPS + i) * 2 + r + 1) * HB, :] for q in range(CHIPS) for r in halves], axis=1)
        gwout[i * HB:(i + 1) * HB, :] = dot_nn(u_t, dh_flat)
    w_got.append(swap(gwout, swout, wo_s, wo_r))
    for i in range(HSTEPS):
        w_got[i].wait_recv()
        w_got[i].wait_send()
        gwin[i] += swin[i]
        outs.append(pltpu.make_async_copy(gwin.at[i], dwin_out.at[:, part(i, HB)], loc.at[4 + i]))
        outs[-1].start()
    w_got[-1].wait_recv()
    w_got[-1].wait_send()
    gwout[...] += swout[...]
    outs.append(pltpu.make_async_copy(gwout, dwout_out, loc.at[4 + HSTEPS]))
    outs[-1].start()

    for c in sent:
        if not any(c is w for w in w_got):
            c.wait_send()
    for c in outs:
        c.wait()


def scatter_kernel(gcand_hbm, gh_hbm, idx_hbm, bounds_hbm, dwin_ref, dwout_ref, grad_out, dwin_out, dwout_out, acc, gcand, gh, idx_sm, bounds_sm, win_b, wout_b, sems):
    ins = [
        pltpu.make_async_copy(src, dst, sems.at[i])
        for i, (src, dst) in enumerate([(idx_hbm, idx_sm), (bounds_hbm, bounds_sm), (gcand_hbm, gcand), (gh_hbm, gh), (dwin_ref, win_b), (dwout_ref, wout_b)])
    ]
    for c in ins:
        c.start()

    @pl.loop(0, ROWS // KC)
    def _(i):
        acc[part(i, KC), :] = jnp.zeros((KC, EMB), F32)

    for c in ins[:3]:
        c.wait()

    @pl.loop(0, CAND // LANES)
    def _(i):
        for v in range(LANES):
            acc[row(idx_sm[DEVS + i // 2, i % 2, v]), :] = gcand[row(i * LANES + v), :]

    for c in ins[3:]:
        c.wait()
    outs = [pltpu.make_async_copy(win_b, dwin_out, sems.at[6]), pltpu.make_async_copy(wout_b, dwout_out, sems.at[7])]
    for c in outs:
        c.start()

    @pl.loop(0, DEVS)
    def _(s):
        def add(i, carry):
            for v in range(CROW):
                r = idx_sm[s, i >> 4, (i & 15) * CROW + v]
                acc[row(r), :] += gh[row(s * TOK + i * CROW + v), :]
            return carry

        lax.fori_loop(bounds_sm[s, 0, 0] >> 3, (bounds_sm[s, 0, 1] + 7) >> 3, add, 0)

    outs.append(pltpu.make_async_copy(acc.at[pl.ds(0, ROWS), :], grad_out, sems.at[8]))
    outs[-1].start()
    for c in outs:
        c.wait()


def solution(mesh):
    def local_step(features, w_in, w_out, table_blk, cand_ids, log_q, targets):
        vmem = pl.BlockSpec(memory_space=pltpu.VMEM)
        hbm = pl.BlockSpec(memory_space=pl.ANY)
        dma = pltpu.SemaphoreType.DMA
        sds = jax.ShapeDtypeStruct

        def v(dtype, *shape):
            return pltpu.VMEM(shape, dtype)

        chips = dma((CHIPS,))
        idx_shape = (DEVS + CROW // 2, 2, LANES)
        loss, gcand, gh, idx, bounds, dwin, dwout = pl.pallas_call(
            main_kernel,
            name="main_kernel",
            out_shape=(
                sds((1, 1), F32), sds((CAND, EMB), F32), sds((TOTAL, EMB), F32),
                sds(idx_shape, I32), sds((DEVS, 1, LANES), I32), sds((IN, HID), F32), sds((HID, EMB), F32),
            ),
            in_specs=[vmem] * 4 + [hbm] * 3,
            out_specs=(vmem,) + (hbm,) * 6,
            scratch_shapes=[
                v(BF16, ROWS, EMB),
                v(F32, ROWS + CROW, EMB),
                v(I32, DEVS, 2, LANES),
                v(I32, *idx_shape),
                pltpu.SMEM(idx_shape, I32),
                v(I32, CORES, CROW, LANES),
                v(F32, CORES, CROW, LANES),
                v(BF16, CHIPS, TOK, IN),
                v(BF16, IN, GRP),
                v(BF16, TOK, HID),
                v(BF16, CHIPS, TOK, EMB),
                v(F32, GRP, EMB),
                v(F32, CAND, EMB),
                v(BF16, CORES, CAND, EMB),
                v(BF16, EMB, PAIR),
                v(I32, PAIR, LANES),
                v(F32, PAIR, LANES),
                v(BF16, GRP, EMB),
                v(BF16, GRP, EMB),
                v(F32, CHIPS, EMB, TOK),
                v(F32, CHIPS, PAIR, TOK),
                v(F32, CHIPS, 2, CHIPS, TOK),
                v(F32, CHIPS, TOK),
                v(F32, CHIPS, TOK),
                v(F32, CHIPS, TOK),
                v(F32, CHIPS, TOK),
                v(F32, CHIPS, TOK),
                v(F32, TOTAL, EMB),
                v(F32, CHIPS, EMB, TOK),
                v(F32, CHIPS, EMB, TOK),
                v(BF16, CHIPS, TOK, EMB),
                v(BF16, GRP, HID),
                v(F32, PAIR, EMB),
                v(F32, CAND, EMB),
                v(F32, HSTEPS, IN, HB),
                v(F32, HID, EMB),
                v(F32, HSTEPS, IN, HB),
                v(F32, HID, EMB),
                v(F32, DEVS, 1, TOK),
                v(I32, DEVS, 1, LANES),
                dma((DEVS - 1,)), dma((DEVS,)),
                chips, chips,
                chips, chips,
                dma, dma,
                dma, dma,
                chips, chips,
                chips, chips,
                dma, dma,
                dma, dma,
                chips, chips,
                dma((HSTEPS,)), dma((HSTEPS,)),
                dma, dma,
                dma((DEVS - 1,)), dma((DEVS,)),
                dma((CROW + HSTEPS,)),
            ],
            compiler_params=pltpu.CompilerParams(collective_id=0, has_side_effects=True, vmem_limit_bytes=VMEM_LIMIT),
        )(features, w_in, w_out, targets.reshape(2, LANES), cand_ids.reshape(DEVS, CROW, LANES), log_q.reshape(DEVS, CROW, LANES), table_blk)
        grad_blk, grad_in, grad_out = pl.pallas_call(
            scatter_kernel,
            name="scatter_kernel",
            out_shape=(sds((ROWS, EMB), F32), sds((IN, HID), F32), sds((HID, EMB), F32)),
            in_specs=[hbm] * 6,
            out_specs=(hbm,) * 3,
            scratch_shapes=[
                v(F32, ROWS + CROW, EMB),
                v(F32, CAND, EMB),
                v(F32, TOTAL, EMB),
                pltpu.SMEM(idx_shape, I32),
                pltpu.SMEM((DEVS, 1, LANES), I32),
                v(F32, IN, HID),
                v(F32, HID, EMB),
                dma((9,)),
            ],
            compiler_params=pltpu.CompilerParams(vmem_limit_bytes=VMEM_LIMIT),
        )(gcand, gh, idx, bounds, dwin, dwout)
        return loss[0, 0], grad_blk, grad_in, grad_out

    return jax.shard_map(local_step, mesh=mesh, in_specs=(P("dp", None), P(), P(), P("dp", None), P(), P(), P("dp")), out_specs=(P(), P("dp", None), P(), P()), check_vma=False)
```

time: 323 us -> 90.2 us (0.28)
  blocking collectives: 112 us -> 0 us
  Pallas kernels: 0 us -> 87.8 us
  waiting for transfers between devices: 75 us -> 0 us
  other arithmetic: 64.1 us -> 0 us
  local copies, waits for them, and re-layouts: 28.8 us -> 0 us
  matrix products: 26.6 us -> 0 us
  between operations: 15.6 us -> 2.45 us
    pallas_call x0 -> x2, Pallas kernels: none -> 87.8 us  [the longest x1 79.5 us: local_step(): pl.pallas_call(main_kernel, name='main_kernel', out_shape=(sds((1, 1), F3...]
    psum x2 -> x0, blocking collectives: 64.8 us -> none  [the longest x1 32.9 us: local_step(): lax.psum(jnp.sum(jnp.exp(cand_logit - top_val[:, None]), axis=1), 'dp')]
    reduce_scatter x1 -> x0, waiting for transfers between devices: 58.5 us -> none  [local_step(): lax.psum_scatter(dq_part, 'dp', scatter_dimension=0, tiled=True)]
    scatter-add x2 -> x0, other arithmetic: 44.2 us -> none  [local_step(): jnp.zeros(table_blk.shape, jnp.float32).at[cand_index].add(grad_cand)]
    pmax x1 -> x0, blocking collectives: 32.7 us -> none  [local_step(): lax.pmax(jnp.max(cand_logit, axis=1), 'dp')]
    dot_general x7 -> x0, matrix products: 26.6 us -> none  [the longest x1 8.25 us: local_step(): jnp.einsum('td,cd->tc', query_all, cand_rows, preferred_element_type=jnp....]
    gather x2 -> x0, local copies, waits for them, and re-layouts: 19.4 us -> none  [the longest x1 13.8 us: local_step(): tgt_rows = table_blk[tgt_index]]
    psum x1 -> x0, waiting for transfers between devices: 16.5 us -> none  [local_step(): lax.psum(jnp.einsum('ti,tf->if', features, d_pre, preferred_element_type=...]
  transfers between devices with their start and end apart: 3 -> 0, of which waited for: 2 -> 0; matrix products, arithmetic and copies ran while one was open for 22% -> 0% of each run, Pallas kernels for 0% -> 0%
where the time goes in v1:
time: 90.2 us; the launch traced here: 90.3 us
  Pallas kernels  87.8 us (97%)
  between operations  2.45 us (3%)
    pallas_call x1, Pallas kernels, local_step(): pl.pallas_call(main_kernel, name='main_kernel', out_shape=(sds((1, 1), F3...  79.5 us
    pallas_call x1, Pallas kernels, local_step(): pl.pallas_call(scatter_kernel, name='scatter_kernel', out_shape=(sds((ROW...  8.37 us

profile of v1, /device:TPU:0, one launch (start us, length us, event | category | flops | bytes accessed | tf_op | source)
XLA Modules:
  0.0 90.3 jit_solution(5477574000393236839)
XLA Ops:
  0.6 79.5 %main_kernel.1 = (f32[1,1]{1,0:T(1,128)}, f32[1024,128]{1,0:T(8,128)}, f32[4096,128]{1,0:T(8,128)}, s32[20,2,128]{2,1,0:T(2,128)}, s32[16,1,128]{2,1,0:T(1,128)}...) custom-call(bf16[256,256]{1,0:T(8,128)(2,1)} %x_ref.1, bf16[256,1024]{1,0:T(8,128)(2,1)} %w_in_ref.1, ...), custom_call_target="tpu_custom_call" | custom-call | tf_op jit(solution)/shard_map/main_kernel/pallas_call | solution.py:477
  80.1 8.4 %scatter_kernel.1 = (f32[16384,128]{1,0:T(8,128)}, f32[256,1024]{1,0:T(8,128)}, f32[1024,128]{1,0:T(8,128)}) custom-call(f32[1024,128]{1,0:T(8,128)} %get-tuple-element.15.gcand_hbm, f32[4096,128]{1,0:T(8,128)} %get-tuple-element.16.gh_hbm, s32[20,2,128]{2,1,0:T(2,128)} %get-tuple-element.17.idx_hbm, s32[16,1,128]{2,1,0:T(1,128)} %get-tuple-element.18.bounds_hbm, ...), custom_call_target="tpu_custom_call" | custom-call | tf_op jit(solution)/shard_map/scatter_kernel/pallas_call | solution.py:544

commit v2 on v1

--- a/solution.py
+++ b/solution.py
@@ -26,7 +26,6 @@
 ROWS = 16384
 TOTAL = 4096
 KC = 256
-STEPS = PAIR // KC
 HB = 256
 HSTEPS = HID // HB
 ROOT_2_PI = 0.7978845608028654
@@ -229,37 +228,28 @@
             cid_b[at:at + LANES, :] = column_of(cand_vm[b, r:r + 1, :])
             lq_b[at:at + LANES, :] = column_of(logq_vm[b, r:r + 1, :])
     e_copy.wait_recv()
-    for i in range(STEPS):
-        b, r = i // (CAND // KC), i % (CAND // KC)
-        e_t[:, i * KC:(i + 1) * KC] = e_all[b, r * KC:(r + 1) * KC, :].T
+    for b in range(CORES):
+        e_t[:, b * CAND:(b + 1) * CAND] = e_all[b].T
     tr_copy.wait_recv()
 
     def twice(x):
         return jnp.concatenate([x, x], axis=1)
 
     def fold(x):
-        return x.reshape(KC // 8, 8, TOK)
+        return x.reshape(PAIR // 8, 8, TOK)
 
     def stats_of(q):
         h = hall[q]
         ids = tall[core * CHIPS + q]
         y_row = jnp.concatenate([ids[r:r + 1, :] for r in halves], axis=1)
 
-        def first(i, top):
-            e_blk = e_all[i // (CAND // KC), part(i % (CAND // KC), KC), :]
-            s = dot_nt(e_blk, h) - twice(lq_b[part(i, KC), :])
-            s = jnp.where(twice(cid_b[part(i, KC), :]) == y_row, -1e9, s)
-            ex_ref[q, part(i, KC), :] = s
-            return jnp.maximum(top, jnp.max(fold(s), axis=0))
-
-        top = top_of(lax.fori_loop(0, STEPS, first, jnp.full((8, TOK), -jnp.inf, F32)))
-
-        def second(i, tot):
-            e = jnp.exp(ex_ref[q, part(i, KC), :] - top)
-            ex_ref[q, part(i, KC), :] = e
-            return tot + jnp.sum(fold(e), axis=0)
-
-        tot = sum_of(lax.fori_loop(0, STEPS, second, jnp.zeros((8, TOK), F32)))
+        s = dot_nt(e_all[...].reshape(PAIR, EMB), h) - twice(lq_b[...])
+        s = jnp.where(twice(cid_b[...]) == y_row, -1e9, s)
+        ex_ref[q] = s
+        top = top_of(jnp.max(fold(s), axis=0))
+        e = jnp.exp(ex_ref[q] - top)
+        ex_ref[q] = e
+        tot = sum_of(jnp.sum(fold(e), axis=0))
         rows = rows_f[part(q, TOK), :] + trow_o[part(q, TOK), :].astype(F32)
         tr_t[q] = rows.T
         z = sum_of((rows * h.astype(F32)).T)
@@ -281,19 +271,15 @@
         x = xs_all[q]
         xt_ref[:, part(q, TOK)] = x.T
 
-        def step(i, carry):
-            act = dot_nn(x, w_in_ref[:, part(i, HB)])
-            tanh = tanh_of(act)
-            cdf = 0.5 * (1.0 + tanh)
-            slope = cdf + act * (0.5 * (1.0 - tanh * tanh)) * (ROOT_2_PI * (1.0 + 3.0 * CUBE * (act * act)))
-            u_t = (act * cdf).T.astype(BF16)
-            for r in halves:
-                at = (q * HSTEPS + i) * 2 + r
-                tab_f[part(at, TOK), :] = slope[:, r * HALF:(r + 1) * HALF]
-                tab_b[part(at, HB), :] = u_t[:, r * HALF:(r + 1) * HALF]
-            return carry
-
-        lax.fori_loop(0, HSTEPS, step, 0)
+        act = dot_nn(x, w_in_ref[...])
+        tanh = tanh_of(act)
+        cdf = 0.5 * (1.0 + tanh)
+        slope = cdf + act * (0.5 * (1.0 - tanh * tanh)) * (ROOT_2_PI * (1.0 + 3.0 * CUBE * (act * act)))
+        u_t = (act * cdf).astype(BF16).T
+        for i in range(HID // LANES):
+            tab_f[part(q * (HID // LANES) + i, TOK), :] = slope[:, i * LANES:(i + 1) * LANES]
+        for r in halves:
+            tab_b[part(q * 2 + r, HID), :] = u_t[:, r * HALF:(r + 1) * HALF]
 
     tower_of(chip)
     for k in NEAR[:3]:
@@ -321,16 +307,10 @@
         h = hall[q]
         f_row = f_ref[row(q), :]
 
-        def body(i, acc):
-            p = (ex_ref[q, part(i, KC), :] * f_row).astype(BF16)
-            de = dot_nn(p, h)
-            if is_first:
-                de_acc[part(i, KC), :] = de
-            else:
-                de_acc[part(i, KC), :] += de
-            return acc + dot_nn(e_t[:, part(i, KC)], p)
-
-        dh_acc[q] = lax.fori_loop(0, STEPS, body, g_ref[row(q), :] * tr_t[q])
+        p = (ex_ref[q] * f_row).astype(BF16)
+        dh_acc[q] = dot_nn(e_t[...], p) + g_ref[row(q), :] * tr_t[q]
+        de = dot_nn(p, h)
+        de_acc[...] = de if is_first else de_acc[...] + de
 
     dh_got = arrivals(dh_in, dh_s, dh_r)
     for k in FAR:
@@ -379,13 +359,9 @@
     def back_of(q):
         dh = dhb_all[q]
 
-        def step(i, carry):
-            e = dot_nt(dh, w_out_ref[part(i, HB), :])
-            slope = [tab_f[part((q * HSTEPS + i) * 2 + r, TOK), :] for r in halves]
-            da_ref[part(q, TOK), part(i, HB)] = (jnp.concatenate(slope, axis=1) * e).astype(BF16)
-            return carry
-
-        lax.fori_loop(0, HSTEPS, step, 0)
+        e = dot_nt(dh, w_out_ref[...])
+        slope = [tab_f[part(q * (HID // LANES) + i, TOK), :] for i in range(HID // LANES)]
+        da_ref[part(q, TOK), :] = (jnp.concatenate(slope, axis=1) * e).astype(BF16)
 
     back_of(chip)
     for k in FAR:
@@ -398,7 +374,7 @@
         w_got.append(swap(gwin.at[i], swin.at[i], wi_s.at[i], wi_r.at[i]))
     dh_flat = dhb_all[...].reshape(GRP, EMB)
     for i in range(HSTEPS):
-        u_t = jnp.concatenate([tab_b[((q * HSTEPS + i) * 2 + r) * HB:((q * HSTEPS + i) * 2 + r + 1) * HB, :] for q in range(CHIPS) for r in halves], axis=1)
+        u_t = jnp.concatenate([tab_b[(q * 2 + r) * HID + i * HB:(q * 2 + r) * HID + (i + 1) * HB, :] for q in range(CHIPS) for r in halves], axis=1)
         gwout[i * HB:(i + 1) * HB, :] = dot_nn(u_t, dh_flat)
     w_got.append(swap(gwout, swout, wo_s, wo_r))
     for i in range(HSTEPS):

time: 90.2 us -> 72.7 us (0.81)
  Pallas kernels: 87.8 us -> 70 us
    pallas_call x1, Pallas kernels: 79.5 us -> 62 us  [local_step(): pl.pallas_call(main_kernel, name='main_kernel', out_shape=(sds((1, 1), F3...]
where the time goes in v2:
time: 72.7 us; the launch traced here: 72.5 us
  Pallas kernels  70 us (96%)
  between operations  2.45 us (3%)
    pallas_call x1, Pallas kernels, local_step(): pl.pallas_call(main_kernel, name='main_kernel', out_shape=(sds((1, 1), F3...  62 us
    pallas_call x1, Pallas kernels, local_step(): pl.pallas_call(scatter_kernel, name='scatter_kernel', out_shape=(sds((ROW...  8.05 us

profile of v2, /device:TPU:0, one launch (start us, length us, event | category | flops | bytes accessed | tf_op | source)
XLA Modules:
  0.0 72.5 jit_solution(1090756346114386954)
XLA Ops:
  0.6 62.0 %main_kernel.1 = (f32[1,1]{1,0:T(1,128)}, f32[1024,128]{1,0:T(8,128)}, f32[4096,128]{1,0:T(8,128)}, s32[20,2,128]{2,1,0:T(2,128)}, s32[16,1,128]{2,1,0:T(1,128)}...) custom-call(bf16[256,256]{1,0:T(8,128)(2,1)} %x_ref.1, bf16[256,1024]{1,0:T(8,128)(2,1)} %w_in_ref.1, ...), custom_call_target="tpu_custom_call" | custom-call | tf_op jit(solution)/shard_map/main_kernel/pallas_call | solution.py:453
  62.6 8.0 %scatter_kernel.1 = (f32[16384,128]{1,0:T(8,128)}, f32[256,1024]{1,0:T(8,128)}, f32[1024,128]{1,0:T(8,128)}) custom-call(f32[1024,128]{1,0:T(8,128)} %get-tuple-element.15.gcand_hbm, f32[4096,128]{1,0:T(8,128)} %get-tuple-element.16.gh_hbm, s32[20,2,128]{2,1,0:T(2,128)} %get-tuple-element.17.idx_hbm, s32[16,1,128]{2,1,0:T(1,128)} %get-tuple-element.18.bounds_hbm, ...), custom_call_target="tpu_custom_call" | custom-call | tf_op jit(solution)/shard_map/scatter_kernel/pallas_call | solution.py:520

commit v3 on v2

--- a/solution.py
+++ b/solution.py
@@ -70,9 +70,9 @@
 
 
 def main_kernel(
-    x_ref, w_in_ref, w_out_ref, tgt_ref, cand_hbm, logq_hbm, table_hbm,
+    x_hbm, w_in_hbm, w_out_hbm, tgt_hbm, cand_hbm, logq_hbm, table_hbm,
     loss_out, gcand_out, gh_out, idx_out, bounds_out, dwin_out, dwout_out,
-    tab_b, tab_f, tall, idx_vm, idx_sm, cand_vm, logq_vm, xs_all, xt_ref, u_ref, hall,
+    x_ref, w_in_ref, w_out_ref, tgt_ref, tab_b, tab_f, tall, idx_vm, idx_sm, cand_vm, logq_vm, xs_all, xt_ref, u_ref, hall,
     rows_f, cand_f, e_all, e_t, cid_b, lq_b, trow_s, trow_o, tr_t,
     ex_ref, st_all, mloc_ref, z_ref, l_ref, f_ref, g_ref, gh_ref,
     dh_acc, dh_in, dhb_all, da_ref, de_acc, de_in, gwin, gwout, swin, swout, loss_all, bounds_vm,
@@ -85,6 +85,7 @@
     oth = 1 - core
     sib = chip * CORES + oth
     base = me * ROWS
+    zc = chip // (CHIPS // 2)
     first_row = chip * (CORES * ROWS)
 
     def flip(k):
@@ -136,6 +137,10 @@
         pl.semaphore_signal(barrier, inc=1, device_id=(dev,), device_id_type=MESH)
 
     chip_blocks = pl.ds(chip * CORES, CORES)
+    inputs = [(tgt_hbm, tgt_ref), (x_hbm, x_ref), (w_in_hbm, w_in_ref), (w_out_hbm, w_out_ref)]
+    inputs = [pltpu.make_async_copy(src, dst, loc.at[3 + i]) for i, (src, dst) in enumerate(inputs)]
+    for c in inputs:
+        c.start()
     early = [
         pltpu.make_async_copy(cand_hbm.at[chip_blocks], cand_vm, loc.at[0]),
         pltpu.make_async_copy(logq_hbm.at[chip_blocks], logq_vm, loc.at[1]),
@@ -143,6 +148,7 @@
     ]
     for c in early:
         c.start()
+    inputs[0].wait()
 
     lane = lax.broadcasted_iota(I32, (1, LANES), 1)
     halves = range(TOK // HALF)
@@ -158,14 +164,16 @@
         line = sum(sum_of(m[r * HALF:(r + 1) * HALF, :].T) for m in moved)
         tall[row(my_slot), row(r), :] = line.astype(I32).reshape(1, 1, LANES)
 
-    pl.semaphore_wait(barrier, DEVS - 1)
-    tgt_got = to_all(tall, my_slot, tgt_s, tgt_r, slot_of)
-
+    for c in inputs[1:]:
+        c.wait()
     xs = dot_nn(perm, x_ref[...]).astype(BF16)
     xs_all[row(chip)] = xs.reshape(1, TOK, IN)
     act = dot_nn(xs, w_in_ref[...])
     u_ref[...] = (act * (0.5 * (1.0 + tanh_of(act)))).astype(BF16)
     hall[row(chip)] = dot_nn(u_ref[...], w_out_ref[...]).astype(BF16).reshape(1, TOK, EMB)
+
+    pl.semaphore_wait(barrier, DEVS - 1)
+    tgt_got = to_all(tall, my_slot, tgt_s, tgt_r, slot_of)
     h_got = spread(hall, h_s, h_r, NEAR)
     x_got = spread(xs_all, x_s, x_r, NEAR)
 
@@ -228,8 +236,6 @@
             cid_b[at:at + LANES, :] = column_of(cand_vm[b, r:r + 1, :])
             lq_b[at:at + LANES, :] = column_of(logq_vm[b, r:r + 1, :])
     e_copy.wait_recv()
-    for b in range(CORES):
-        e_t[:, b * CAND:(b + 1) * CAND] = e_all[b].T
     tr_copy.wait_recv()
 
     def twice(x):
@@ -281,6 +287,8 @@
         for r in halves:
             tab_b[part(q * 2 + r, HID), :] = u_t[:, r * HALF:(r + 1) * HALF]
 
+    for b in range(CORES):
+        e_t[:, b * CAND:(b + 1) * CAND] = e_all[b].T
     tower_of(chip)
     for k in NEAR[:3]:
         x_got[k].wait_recv()
@@ -312,10 +320,35 @@
         de = dot_nn(p, h)
         de_acc[...] = de if is_first else de_acc[...] + de
 
-    dh_got = arrivals(dh_in, dh_s, dh_r)
-    for k in FAR:
+    parts = [pl.ds(r * (EMB // 2), EMB // 2) for r in range(2)]
+    JOIN = {7: (1, 6), 6: (2, 4), 5: (4, 1), 3: (1, 2), 4: (4, 0), 1: (1, 0), 2: (2, 0)}
+
+    def pass_on(k, r):
+        link = JOIN[k][0]
+        go(rcopy(dh_acc.at[peers[k], parts[r], :], dh_in.at[k, parts[r], :], dh_s.at[r, k], dh_r.at[r, k], peers[link] * CORES + core))
+
+    def join(k, r):
+        link, into = JOIN[k]
+        rcopy(dh_in.at[k, parts[r], :], dh_in.at[k, parts[r], :], dh_s.at[r, k], dh_r.at[r, k], peers[link] * CORES + core).wait_recv()
+        place = peers[into] if into else chip
+        dh_acc[place, parts[r], :] += dh_in[k, parts[r], :]
+
+    def relay(k, r):
+        join(k, r)
+        pass_on(JOIN[k][1], r)
+
+    for k in (7, 6, 3, 5, 4):
         grads_of(peers[k], k == FAR[0])
-        go(rcopy(dh_acc.at[peers[k]], dh_in.at[chip], dh_s.at[k], dh_r.at[chip], peers[k] * CORES + core))
+        if k in (7, 3, 5):
+            pass_on(k, 0)
+            pass_on(k, 1)
+    relay(7, 0)
+    grads_of(peers[1], False)
+    grads_of(peers[2], False)
+    relay(7, 1)
+    for r in range(2):
+        for k in (5, 3, 6):
+            relay(k, r)
     grads_of(chip, False)
     de_copy = swap(de_acc.at[part(oth, CAND), :], de_in, de_s, de_r)
 
@@ -348,13 +381,12 @@
     for c in outs:
         c.start()
 
-    for k in NEAR:
-        dh_got[k].wait_recv()
+    for k in (2, 1, 4):
+        for r in range(2):
+            join(k, r)
     total = dh_acc[chip]
-    for k in NEAR:
-        total = total + dh_in[peers[k]]
     dhb_all[row(chip)] = total.T.astype(BF16).reshape(1, TOK, EMB)
-    db_got = spread(dhb_all, db_s, db_r, FAR)
+    db_got = spread(dhb_all, db_s, db_r, (7, 6, 5, 4, 3, 2, 1))
 
     def back_of(q):
         dh = dhb_all[q]
@@ -363,19 +395,27 @@
         slope = [tab_f[part(q * (HID // LANES) + i, TOK), :] for i in range(HID // LANES)]
         da_ref[part(q, TOK), :] = (jnp.concatenate(slope, axis=1) * e).astype(BF16)
 
-    back_of(chip)
-    for k in FAR:
-        db_got[k].wait_recv()
-        back_of(peers[k])
-
     w_got = []
-    for i in range(HSTEPS):
-        gwin[i] = dot_nn(xt_ref[...], da_ref[:, i * HB:(i + 1) * HB])
-        w_got.append(swap(gwin.at[i], swin.at[i], wi_s.at[i], wi_r.at[i]))
-    dh_flat = dhb_all[...].reshape(GRP, EMB)
-    for i in range(HSTEPS):
-        u_t = jnp.concatenate([tab_b[(q * 2 + r) * HID + i * HB:(q * 2 + r) * HID + (i + 1) * HB, :] for q in range(CHIPS) for r in halves], axis=1)
-        gwout[i * HB:(i + 1) * HB, :] = dot_nn(u_t, dh_flat)
+    for half, ks in enumerate(((7, 6, 5, 4), (3, 2, 1, 0))):
+        for k in ks:
+            if k:
+                db_got[k].wait_recv()
+            back_of(peers[k] if k else chip)
+        z_side = zc if half else 1 - zc
+        xt = xt_ref[:, part(z_side, GRP // 2)]
+        for i in range(HSTEPS):
+            new = dot_nn(xt, da_ref[part(z_side, GRP // 2), i * HB:(i + 1) * HB])
+            gwin[i] = gwin[i] + new if half else new
+            if half:
+                w_got.append(swap(gwin.at[i], swin.at[i], wi_s.at[i], wi_r.at[i]))
+        near = CHIPS // 2
+        dh_flat = dhb_all[pl.ds(z_side * near, near)].reshape(GRP // 2, EMB)
+        for i in range(HSTEPS):
+            at = [((z_side * near + q) * 2 + r) * HID + i * HB for q in range(near) for r in halves]
+            u_t = jnp.concatenate([tab_b[pl.ds(pl.multiple_of(a, HB), HB), :] for a in at], axis=1)
+            new = dot_nn(u_t, dh_flat)
+            here = gwout.at[i * HB:(i + 1) * HB, :]
+            here[...] = here[...] + new if half else new
     w_got.append(swap(gwout, swout, wo_s, wo_r))
     for i in range(HSTEPS):
         w_got[i].wait_recv()
@@ -457,9 +497,13 @@
                 sds((1, 1), F32), sds((CAND, EMB), F32), sds((TOTAL, EMB), F32),
                 sds(idx_shape, I32), sds((DEVS, 1, LANES), I32), sds((IN, HID), F32), sds((HID, EMB), F32),
             ),
-            in_specs=[vmem] * 4 + [hbm] * 3,
+            in_specs=[hbm] * 7,
             out_specs=(vmem,) + (hbm,) * 6,
             scratch_shapes=[
+                v(BF16, TOK, IN),
+                v(BF16, IN, HID),
+                v(BF16, HID, EMB),
+                v(I32, 2, LANES),
                 v(BF16, ROWS, EMB),
                 v(F32, ROWS + CROW, EMB),
                 v(I32, DEVS, 2, LANES),
@@ -506,7 +550,7 @@
                 dma, dma,
                 dma, dma,
                 chips, chips,
-                chips, chips,
+                dma((2, CHIPS)), dma((2, CHIPS)),
                 dma, dma,
                 dma, dma,
                 chips, chips,

time: 72.7 us -> 69.9 us (0.961)
  Pallas kernels: 70 us -> 67.2 us
    pallas_call x1, Pallas kernels: 62 us -> 59.2 us  [local_step(): pl.pallas_call(main_kernel, name='main_kernel', out_shape=(sds((1, 1), F3...]
where the time goes in v3:
time: 69.9 us; the launch traced here: 69.7 us
  Pallas kernels  67.2 us (96%)
  between operations  2.45 us (4%)
    pallas_call x1, Pallas kernels, local_step(): pl.pallas_call(main_kernel, name='main_kernel', out_shape=(sds((1, 1), F3...  59.2 us
    pallas_call x1, Pallas kernels, local_step(): pl.pallas_call(scatter_kernel, name='scatter_kernel', out_shape=(sds((ROW...  7.98 us

profile of v3, /device:TPU:0, one launch (start us, length us, event | category | flops | bytes accessed | tf_op | source)
XLA Modules:
  0.0 69.7 jit_solution(16864734828028280346)
XLA Ops:
  0.6 59.2 %main_kernel.1 = (f32[1,1]{1,0:T(1,128)}, f32[1024,128]{1,0:T(8,128)}, f32[4096,128]{1,0:T(8,128)}, s32[20,2,128]{2,1,0:T(2,128)}, s32[16,1,128]{2,1,0:T(1,128)}...) custom-call(bf16[256,256]{1,0:T(8,128)(2,1)} %x_hbm.1, bf16[256,1024]{1,0:T(8,128)(2,1)} %w_in_hbm.1, ...), custom_call_target="tpu_custom_call" | custom-call | tf_op jit(solution)/shard_map/main_kernel/pallas_call | solution.py:493
  59.9 8.0 %scatter_kernel.1 = (f32[16384,128]{1,0:T(8,128)}, f32[256,1024]{1,0:T(8,128)}, f32[1024,128]{1,0:T(8,128)}) custom-call(f32[1024,128]{1,0:T(8,128)} %get-tuple-element.15.gcand_hbm, f32[4096,128]{1,0:T(8,128)} %get-tuple-element.16.gh_hbm, s32[20,2,128]{2,1,0:T(2,128)} %get-tuple-element.17.idx_hbm, s32[16,1,128]{2,1,0:T(1,128)} %get-tuple-element.18.bounds_hbm, ...), custom_call_target="tpu_custom_call" | custom-call | tf_op jit(solution)/shard_map/scatter_kernel/pallas_call | solution.py:564

commit v4 on v3

--- a/solution.py
+++ b/solution.py
@@ -35,6 +35,8 @@
 
 NEAR = (1, 2, 4, 3, 5, 6, 7)
 FAR = (7, 6, 5, 3, 4, 2, 1)
+DOWN = (7, 6, 5, 4, 3, 2, 1)
+TOWERS = (3, 5, 6, 7, 4, 2, 1)
 
 
 def dot_nt(lhs, rhs):
@@ -175,7 +177,7 @@
     pl.semaphore_wait(barrier, DEVS - 1)
     tgt_got = to_all(tall, my_slot, tgt_s, tgt_r, slot_of)
     h_got = spread(hall, h_s, h_r, NEAR)
-    x_got = spread(xs_all, x_s, x_r, NEAR)
+    x_got = spread(xs_all, x_s, x_r, (3, 5, 6, 7))
 
     for c in early:
         c.wait()
@@ -213,7 +215,7 @@
         return jnp.sum(jnp.sum(mask.astype(F32), axis=2, keepdims=True), axis=1, keepdims=True)
 
     lane3 = lax.broadcasted_iota(I32, (DEVS, 1, LANES), 2)
-    bounds_vm[...] = jnp.where(lane3 == 0, count(loc_idx < 0), count(loc_idx < ROWS)).astype(I32)
+    bounds_vm[...] = jnp.where(lane3 == 0, count(loc_idx < 0), jnp.where(lane3 == 1, count(loc_idx < ROWS // 2), count(loc_idx < ROWS))).astype(I32)
     tok_at = pl.ds(0, DEVS)
     idx_copy = pltpu.make_async_copy(idx_vm.at[tok_at], idx_sm.at[tok_at], loc.at[0])
     idx_copy.start()
@@ -267,10 +269,12 @@
         st_all[row(chip), 0, row(q), :] = both.reshape(1, 1, TOK)
         st_all[row(chip), 1, row(q), :] = tot.reshape(1, 1, TOK)
 
-    stats_of(chip)
-    for k in NEAR:
-        h_got[k].wait_recv()
-        stats_of(peers[k])
+    for pair in ((0, 1), (2, 4), (3, 5), (6, 7)):
+        for k in pair:
+            if k:
+                h_got[k].wait_recv()
+        for k in pair:
+            stats_of(peers[k] if k else chip)
     st_got = spread(st_all, st_s, st_r, FAR)
 
     def tower_of(q):
@@ -289,10 +293,13 @@
 
     for b in range(CORES):
         e_t[:, b * CAND:(b + 1) * CAND] = e_all[b].T
-    tower_of(chip)
-    for k in NEAR[:3]:
+    def late_tower(k):
         x_got[k].wait_recv()
         tower_of(peers[k])
+
+    tower_of(chip)
+    for k in TOWERS[:3]:
+        late_tower(k)
 
     for k in NEAR:
         st_got[k].wait_recv()
@@ -320,18 +327,18 @@
         de = dot_nn(p, h)
         de_acc[...] = de if is_first else de_acc[...] + de
 
-    parts = [pl.ds(r * (EMB // 2), EMB // 2) for r in range(2)]
+    parts = [pl.ds(r * HALF, HALF) for r in halves]
     JOIN = {7: (1, 6), 6: (2, 4), 5: (4, 1), 3: (1, 2), 4: (4, 0), 1: (1, 0), 2: (2, 0)}
 
     def pass_on(k, r):
         link = JOIN[k][0]
-        go(rcopy(dh_acc.at[peers[k], parts[r], :], dh_in.at[k, parts[r], :], dh_s.at[r, k], dh_r.at[r, k], peers[link] * CORES + core))
+        go(rcopy(dh_acc.at[peers[k], :, parts[r]], dh_in.at[k, :, parts[r]], dh_s.at[r, k], dh_r.at[r, k], peers[link] * CORES + core))
 
     def join(k, r):
         link, into = JOIN[k]
-        rcopy(dh_in.at[k, parts[r], :], dh_in.at[k, parts[r], :], dh_s.at[r, k], dh_r.at[r, k], peers[link] * CORES + core).wait_recv()
+        rcopy(dh_in.at[k, :, parts[r]], dh_in.at[k, :, parts[r]], dh_s.at[r, k], dh_r.at[r, k], peers[link] * CORES + core).wait_recv()
         place = peers[into] if into else chip
-        dh_acc[place, parts[r], :] += dh_in[k, parts[r], :]
+        dh_acc[place, :, parts[r]] += dh_in[k, :, parts[r]]
 
     def relay(k, r):
         join(k, r)
@@ -352,6 +359,9 @@
     grads_of(chip, False)
     de_copy = swap(de_acc.at[part(oth, CAND), :], de_in, de_s, de_r)
 
+
+    for k in (1, 2, 4):
+        go(rcopy(xs_all.at[chip], xs_all.at[chip], x_s.at[k], x_r.at[chip], peers[k] * CORES + core))
     @pl.loop(0, CHIPS)
     def _(q):
         g_row = g_ref[row(q), :]
@@ -360,10 +370,20 @@
             gh_ref[part((core * CHIPS + q) * 2 + r, HALF), :] = col * hall[q, r * HALF:(r + 1) * HALF, :].astype(F32)
 
     gh_copy = swap(gh_ref.at[part(core, GRP), :], gh_ref.at[part(core, GRP), :], gh_s, gh_r)
-
-    for k in NEAR[3:]:
-        x_got[k].wait_recv()
-        tower_of(peers[k])
+    late_tower(TOWERS[3])
+
+    db_got = {}
+    for r in halves:
+        for k in (2, 1, 4):
+            join(k, r)
+        dhb_all[row(chip), parts[r], :] = dh_acc[chip, :, parts[r]].T.astype(BF16).reshape(1, HALF, EMB)
+        for k in DOWN:
+            here, there = dhb_all.at[chip, parts[r], :], dhb_all.at[peers[k], parts[r], :]
+            dev = peers[k] * CORES + core
+            db_got[r, k] = rcopy(there, there, db_s.at[r, k], db_r.at[r, peers[k]], dev)
+            go(rcopy(here, here, db_s.at[r, k], db_r.at[r, chip], dev))
+    for k in TOWERS[4:]:
+        late_tower(k)
 
     de_copy.wait_recv()
     for r in range(CAND // KC):
@@ -381,13 +401,6 @@
     for c in outs:
         c.start()
 
-    for k in (2, 1, 4):
-        for r in range(2):
-            join(k, r)
-    total = dh_acc[chip]
-    dhb_all[row(chip)] = total.T.astype(BF16).reshape(1, TOK, EMB)
-    db_got = spread(dhb_all, db_s, db_r, (7, 6, 5, 4, 3, 2, 1))
-
     def back_of(q):
         dh = dhb_all[q]
 
@@ -396,10 +409,11 @@
         da_ref[part(q, TOK), :] = (jnp.concatenate(slope, axis=1) * e).astype(BF16)
 
     w_got = []
-    for half, ks in enumerate(((7, 6, 5, 4), (3, 2, 1, 0))):
+    for half, ks in enumerate(((7, 6, 5, 4), (0, 3, 2, 1))):
         for k in ks:
             if k:
-                db_got[k].wait_recv()
+                for r in halves:
+                    db_got[r, k].wait_recv()
             back_of(peers[k] if k else chip)
         z_side = zc if half else 1 - zc
         xt = xt_ref[:, part(z_side, GRP // 2)]
@@ -416,15 +430,17 @@
             new = dot_nn(u_t, dh_flat)
             here = gwout.at[i * HB:(i + 1) * HB, :]
             here[...] = here[...] + new if half else new
-    w_got.append(swap(gwout, swout, wo_s, wo_r))
+            if half:
+                w_got.append(swap(here, swout.at[i * HB:(i + 1) * HB, :], wo_s.at[i], wo_r.at[i]))
     for i in range(HSTEPS):
         w_got[i].wait_recv()
         w_got[i].wait_send()
         gwin[i] += swin[i]
         outs.append(pltpu.make_async_copy(gwin.at[i], dwin_out.at[:, part(i, HB)], loc.at[4 + i]))
         outs[-1].start()
-    w_got[-1].wait_recv()
-    w_got[-1].wait_send()
+    for c in w_got[HSTEPS:]:
+        c.wait_recv()
+        c.wait_send()
     gwout[...] += swout[...]
     outs.append(pltpu.make_async_copy(gwout, dwout_out, loc.at[4 + HSTEPS]))
     outs[-1].start()
@@ -462,18 +478,23 @@
     for c in outs:
         c.start()
 
-    @pl.loop(0, DEVS)
-    def _(s):
-        def add(i, carry):
-            for v in range(CROW):
-                r = idx_sm[s, i >> 4, (i & 15) * CROW + v]
-                acc[row(r), :] += gh[row(s * TOK + i * CROW + v), :]
-            return carry
-
-        lax.fori_loop(bounds_sm[s, 0, 0] >> 3, (bounds_sm[s, 0, 1] + 7) >> 3, add, 0)
-
-    outs.append(pltpu.make_async_copy(acc.at[pl.ds(0, ROWS), :], grad_out, sems.at[8]))
-    outs[-1].start()
+    for half in range(2):
+
+        @pl.loop(0, DEVS)
+        def _(s):
+            def add(i, carry):
+                for v in range(CROW):
+                    r = idx_sm[s, i >> 4, (i & 15) * CROW + v]
+                    acc[row(r), :] += gh[row(s * TOK + i * CROW + v), :]
+                return carry
+
+            first, last = bounds_sm[s, 0, half], bounds_sm[s, 0, half + 1]
+            first = (first + 7) >> 3 if half else first >> 3
+            lax.fori_loop(first, (last + 7) >> 3, add, 0)
+
+        rows = pl.ds(half * (ROWS // 2), ROWS // 2)
+        outs.append(pltpu.make_async_copy(acc.at[rows, :], grad_out.at[rows, :], sems.at[8 + half]))
+        outs[-1].start()
     for c in outs:
         c.wait()
 
@@ -553,9 +574,9 @@
                 dma((2, CHIPS)), dma((2, CHIPS)),
                 dma, dma,
                 dma, dma,
-                chips, chips,
+                dma((2, CHIPS)), dma((2, CHIPS)),
                 dma((HSTEPS,)), dma((HSTEPS,)),
-                dma, dma,
+                dma((HSTEPS,)), dma((HSTEPS,)),
                 dma((DEVS - 1,)), dma((DEVS,)),
                 dma((CROW + HSTEPS,)),
             ],
@@ -575,7 +596,7 @@
                 pltpu.SMEM((DEVS, 1, LANES), I32),
                 v(F32, IN, HID),
                 v(F32, HID, EMB),
-                dma((9,)),
+                dma((10,)),
             ],
             compiler_params=pltpu.CompilerParams(vmem_limit_bytes=VMEM_LIMIT),
         )(gcand, gh, idx, bounds, dwin, dwout)

time: 69.9 us -> 67.2 us (0.961)
  Pallas kernels: 67.2 us -> 64.7 us
    pallas_call x1, Pallas kernels: 59.2 us -> 57.1 us  [local_step(): pl.pallas_call(main_kernel, name='main_kernel', out_shape=(sds((1, 1), F3...]
where the time goes in v4:
time: 67.2 us; the launch traced here: 67.1 us
  Pallas kernels  64.7 us (96%)
  between operations  2.45 us (4%)
    pallas_call x1, Pallas kernels, local_step(): pl.pallas_call(main_kernel, name='main_kernel', out_shape=(sds((1, 1), F3...  57.1 us
    pallas_call x1, Pallas kernels, local_step(): pl.pallas_call(scatter_kernel, name='scatter_kernel', out_shape=(sds((ROW...  7.56 us

profile of v4, /device:TPU:0, one launch (start us, length us, event | category | flops | bytes accessed | tf_op | source)
XLA Modules:
  0.0 67.1 jit_solution(14586775084125460219)
XLA Ops:
  0.6 57.1 %main_kernel.1 = (f32[1,1]{1,0:T(1,128)}, f32[1024,128]{1,0:T(8,128)}, f32[4096,128]{1,0:T(8,128)}, s32[20,2,128]{2,1,0:T(2,128)}, s32[16,1,128]{2,1,0:T(1,128)}...) custom-call(bf16[256,256]{1,0:T(8,128)(2,1)} %x_hbm.1, bf16[256,1024]{1,0:T(8,128)(2,1)} %w_in_hbm.1, ...), custom_call_target="tpu_custom_call" | custom-call | tf_op jit(solution)/shard_map/main_kernel/pallas_call | solution.py:514
  57.7 7.6 %scatter_kernel.1 = (f32[16384,128]{1,0:T(8,128)}, f32[256,1024]{1,0:T(8,128)}, f32[1024,128]{1,0:T(8,128)}) custom-call(f32[1024,128]{1,0:T(8,128)} %get-tuple-element.15.gcand_hbm, f32[4096,128]{1,0:T(8,128)} %get-tuple-element.16.gh_hbm, s32[20,2,128]{2,1,0:T(2,128)} %get-tuple-element.17.idx_hbm, s32[16,1,128]{2,1,0:T(1,128)} %get-tuple-element.18.bounds_hbm, ...), custom_call_target="tpu_custom_call" | custom-call | tf_op jit(solution)/shard_map/scatter_kernel/pallas_call | solution.py:585

commit v5 on v4

--- a/solution.py
+++ b/solution.py
@@ -282,9 +282,10 @@
         xt_ref[:, part(q, TOK)] = x.T
 
         act = dot_nn(x, w_in_ref[...])
-        tanh = tanh_of(act)
-        cdf = 0.5 * (1.0 + tanh)
-        slope = cdf + act * (0.5 * (1.0 - tanh * tanh)) * (ROOT_2_PI * (1.0 + 3.0 * CUBE * (act * act)))
+        wide = ROOT_2_PI + (ROOT_2_PI * CUBE) * (act * act)
+        tanh = jnp.tanh(act * wide)
+        cdf = 0.5 + 0.5 * tanh
+        slope = cdf + (act * (cdf * (1.0 - tanh))) * (3.0 * wide - 2.0 * ROOT_2_PI)
         u_t = (act * cdf).astype(BF16).T
         for i in range(HID // LANES):
             tab_f[part(q * (HID // LANES) + i, TOK), :] = slope[:, i * LANES:(i + 1) * LANES]

time: 67.2 us -> 66.8 us (level)
  no operation moved by 1% of the time
where the time goes in v5:
time: 66.8 us; the launch traced here: 66.7 us
  Pallas kernels  64.2 us (96%)
  between operations  2.45 us (4%)
    pallas_call x1, Pallas kernels, local_step(): pl.pallas_call(main_kernel, name='main_kernel', out_shape=(sds((1, 1), F3...  56.7 us
    pallas_call x1, Pallas kernels, local_step(): pl.pallas_call(scatter_kernel, name='scatter_kernel', out_shape=(sds((ROW...  7.46 us

profile of v5, /device:TPU:0, one launch (start us, length us, event | category | flops | bytes accessed | tf_op | source)
XLA Modules:
  0.0 66.7 jit_solution(540653332665684723)
XLA Ops:
  0.6 56.7 %main_kernel.1 = (f32[1,1]{1,0:T(1,128)}, f32[1024,128]{1,0:T(8,128)}, f32[4096,128]{1,0:T(8,128)}, s32[20,2,128]{2,1,0:T(2,128)}, s32[16,1,128]{2,1,0:T(1,128)}...) custom-call(bf16[256,256]{1,0:T(8,128)(2,1)} %x_hbm.1, bf16[256,1024]{1,0:T(8,128)(2,1)} %w_in_hbm.1, ...), custom_call_target="tpu_custom_call" | custom-call | tf_op jit(solution)/shard_map/main_kernel/pallas_call | solution.py:515
  57.4 7.5 %scatter_kernel.1 = (f32[16384,128]{1,0:T(8,128)}, f32[256,1024]{1,0:T(8,128)}, f32[1024,128]{1,0:T(8,128)}) custom-call(f32[1024,128]{1,0:T(8,128)} %get-tuple-element.15.gcand_hbm, f32[4096,128]{1,0:T(8,128)} %get-tuple-element.16.gh_hbm, s32[20,2,128]{2,1,0:T(2,128)} %get-tuple-element.17.idx_hbm, s32[16,1,128]{2,1,0:T(1,128)} %get-tuple-element.18.bounds_hbm, ...), custom_call_target="tpu_custom_call" | custom-call | tf_op jit(solution)/shard_map/scatter_kernel/pallas_call | solution.py:586
